TPU v7x, 32 devices: a whole 2x2x4 slice. The times are simulated.
32 devices in a mesh: dev: 32 (over z, y, x, core).
Axes of the slice: x: 2, y: 2, z: 4, core: 2. Of those that a mesh axis runs over, the one named last changes fastest.
Arguments:
- state: float32 [2, 1048576], P(None, 'dev'), as said below
- angles: float32 [20, 3], replicated, may hold values from -3.140625 to 3.140625
- sample_high: int32 [262144, 1], P('dev'), may hold values from 0 to 31; in each aligned block of 8192 rows (0 to 8191, 8192 to 16383, ...) at most 1024 rows name the same one
- sample_low: int32 [262144], P('dev'), may hold values from 0 to 32767
- marginal_qubits: int32 [10], replicated, may hold values from 0 to 19, as said below
Outputs:
- sample_probs: float32 [262144], P('dev')
- histogram: float32 [1024], P('dev')
- fidelity: float32 [], replicated
Inputs may be any that keep to these rules, and one draw needn't show every extreme that they name: The state is unit noise times a product over qubits of factors between exp(-0.2) and exp(0.2). `marginal_qubits`: 10 different qubit numbers. `sample_high`: among the rows of one device no value occurs more than 1024 times, and in some devices one value occurs exactly 1024 times.
All inputs are finite; a program needn't handle non-finite values.
Results may differ from a plain program's by a relative error of at most 0.00075.
Values sent between devices are 32-bit elements.
A program may use at most 64 MiB of HBM per device.

v0:
```python
import jax
import jax.numpy as jnp
from jax import lax
from jax.sharding import PartitionSpec as P


def gate_parts(angles):
    theta = angles[:, 0]
    first = angles[:, 1]
    second = angles[:, 2]
    cosine = jnp.cos(theta)
    sine = jnp.sin(theta)
    zeros = jnp.zeros_like(cosine)
    real_part = jnp.stack(
        [
            jnp.stack([cosine, -jnp.cos(second) * sine], -1),
            jnp.stack([jnp.cos(first) * sine, jnp.cos(first + second) * cosine], -1),
        ],
        -2,
    )
    imag_part = jnp.stack(
        [
            jnp.stack([zeros, -jnp.sin(second) * sine], -1),
            jnp.stack([jnp.sin(first) * sine, jnp.sin(first + second) * cosine], -1),
        ],
        -2,
    )
    return (real_part, imag_part)


def kron_gates(gate_real, gate_imag, chosen):
    mat_real = gate_real[chosen[0]]
    mat_imag = gate_imag[chosen[0]]
    for qubit in chosen[1:]:
        next_real = jnp.kron(mat_real, gate_real[qubit]) - jnp.kron(mat_imag, gate_imag[qubit])
        next_imag = jnp.kron(mat_real, gate_imag[qubit]) + jnp.kron(mat_imag, gate_real[qubit])
        mat_real, mat_imag = (next_real, next_imag)
    return (mat_real, mat_imag)


def apply_block(mat_real, mat_imag, field_real, field_imag):

    def product(matrix, field):
        return jnp.einsum("ij,hjc->hic", matrix, field, precision=lax.Precision.HIGHEST)

    new_real = product(mat_real, field_real) - product(mat_imag, field_imag)
    new_imag = product(mat_real, field_imag) + product(mat_imag, field_real)
    return (new_real, new_imag)


def lookup_rows(weight_rows, offsets):
    lane_count = weight_rows.shape[1]
    lane_bits = lane_count.bit_length() - 1
    lane_ids = jnp.arange(lane_count, dtype=jnp.int32)

    def one_block(block):
        upper = block >> lane_bits
        lower = block & lane_count - 1
        picked = jnp.take(weight_rows, upper, axis=0)
        return jnp.sum(jnp.where(lower[:, None] == lane_ids[None, :], picked, 0.0), axis=1)

    total = offsets.shape[0]
    if total % 1024 == 0 and total > 1024:
        return lax.map(one_block, offsets.reshape(total // 1024, 1024)).reshape(total)
    return one_block(offsets)


def shards(state, angles, sample_high, sample_low, marginal_qubits):
    devices = lax.axis_size("dev")
    global_bits = devices.bit_length() - 1
    amps_local = state.shape[1]
    local_bits = amps_local.bit_length() - 1
    qubits = local_bits + global_bits
    position = lax.axis_index("dev")
    gate_real, gate_imag = gate_parts(angles)
    real_part = state[0]
    imag_part = state[1]
    for first_qubit in range(0, local_bits, 6):
        width = min(6, local_bits - first_qubit)
        chosen = list(range(first_qubit + width - 1, first_qubit - 1, -1))
        mat_real, mat_imag = kron_gates(gate_real, gate_imag, chosen)
        shape = (amps_local // 2 ** (first_qubit + width), 2**width, 2**first_qubit)
        real_part, imag_part = apply_block(
            mat_real, mat_imag, real_part.reshape(shape), imag_part.reshape(shape)
        )
        real_part = real_part.reshape(amps_local)
        imag_part = imag_part.reshape(amps_local)
    stride = amps_local // devices
    stacked = jnp.stack([real_part, imag_part]).reshape(2, devices, stride)
    swapped = lax.all_to_all(stacked, "dev", split_axis=1, concat_axis=1, tiled=True)
    mat_real, mat_imag = kron_gates(
        gate_real, gate_imag, list(range(qubits - 1, local_bits - 1, -1))
    )
    new_real, new_imag = apply_block(mat_real, mat_imag, swapped[0][None], swapped[1][None])
    restored = lax.all_to_all(
        jnp.stack([new_real[0], new_imag[0]]), "dev", split_axis=1, concat_axis=1, tiled=True
    )
    real_part = restored[0].reshape(amps_local)
    imag_part = restored[1].reshape(amps_local)
    weight = real_part * real_part + imag_part * imag_part
    lane_total = min(128, amps_local)
    weight_rows = weight.reshape(amps_local // lane_total, lane_total)
    norm = lax.psum(jnp.sum(weight), "dev")
    samp_local = sample_low.shape[0]
    owner = sample_high[:, 0]
    capacity = 4 * samp_local // devices
    block_rows = min(512, samp_local)
    block_count = samp_local // block_rows
    owner_hot = (owner[:, None] == jnp.arange(devices, dtype=jnp.int32)[None, :]).astype(
        jnp.float32
    )
    hot_blocks = owner_hot.reshape(block_count, block_rows, devices).astype(jnp.bfloat16)
    row_ids = jnp.arange(block_rows, dtype=jnp.int32)
    earlier = (row_ids[:, None] > row_ids[None, :]).astype(jnp.bfloat16)
    within = jnp.einsum("ij,bjd->bid", earlier, hot_blocks, preferred_element_type=jnp.float32)
    block_totals = jnp.sum(owner_hot.reshape(block_count, block_rows, devices), axis=1)
    block_before = jnp.cumsum(block_totals, axis=0) - block_totals
    ranking = jnp.sum(
        (within + block_before[:, None, :]) * owner_hot.reshape(block_count, block_rows, devices),
        axis=2,
    ).reshape(samp_local)
    rank_hot = (ranking[:, None] == jnp.arange(capacity, dtype=jnp.float32)[None, :]).astype(
        jnp.float32
    )
    shifted_low = (sample_low + 1).astype(jnp.float32)
    placed = jnp.dot(
        (owner_hot * shifted_low[:, None]).T, rank_hot, precision=lax.Precision.HIGHEST
    )
    requests = placed.astype(jnp.int32) - 1
    incoming = lax.all_to_all(requests, "dev", split_axis=0, concat_axis=0, tiled=True)
    found = lookup_rows(weight_rows, jnp.maximum(incoming, 0).reshape(devices * capacity))
    answers = jnp.where(incoming >= 0, found.reshape(devices, capacity), 0.0)
    replies = lax.all_to_all(answers, "dev", split_axis=0, concat_axis=0, tiled=True)
    values = jnp.sum(
        jnp.dot(owner_hot, replies, precision=lax.Precision.HIGHEST) * rank_hot, axis=1
    )
    marg_count = marginal_qubits.shape[0]
    bin_count = 2**marg_count
    per_device = bin_count // devices
    lower_bits = local_bits // 2
    lower_size = 2**lower_bits
    upper_size = amps_local // lower_size
    places = jnp.arange(marg_count, dtype=jnp.int32)
    is_lower = marginal_qubits < lower_bits
    is_upper = (marginal_qubits >= lower_bits) & (marginal_qubits < local_bits)
    is_global = marginal_qubits >= local_bits
    lower_ids = jnp.arange(lower_size, dtype=jnp.int32)
    upper_ids = jnp.arange(upper_size, dtype=jnp.int32)
    lower_code = jnp.sum(
        jnp.where(
            is_lower[None, :],
            (lower_ids[:, None] >> jnp.minimum(marginal_qubits, 30)[None, :] & 1)
            << places[None, :],
            0,
        ),
        axis=1,
    )
    upper_shift = jnp.clip(marginal_qubits - lower_bits, 0, 30)
    upper_code = jnp.sum(
        jnp.where(
            is_upper[None, :],
            (upper_ids[:, None] >> upper_shift[None, :] & 1) << places[None, :],
            0,
        ),
        axis=1,
    )
    global_shift = jnp.clip(marginal_qubits - local_bits, 0, 30)
    global_code = jnp.sum(jnp.where(is_global, (position >> global_shift & 1) << places, 0))
    upper_code = upper_code + global_code
    bin_ids = jnp.arange(bin_count, dtype=jnp.int32)
    lower_hot = (lower_code[:, None] == bin_ids[None, :]).astype(jnp.float32)
    upper_hot = (upper_code[:, None] == bin_ids[None, :]).astype(jnp.float32)
    folded = jnp.dot(
        weight.reshape(upper_size, lower_size), lower_hot, precision=lax.Precision.HIGHEST
    )
    joint = jnp.dot(upper_hot.T, folded, precision=lax.Precision.HIGHEST)
    lower_mask = jnp.sum(jnp.where(is_lower, 1 << places, 0))
    column_ids = bin_ids & lower_mask
    line_ids = bin_ids - column_ids
    partial_value = jnp.take(
        joint.reshape(bin_count * bin_count), line_ids * bin_count + column_ids
    )
    fidelity_part = jnp.sum(values)
    summed_hist, total = lax.psum((partial_value, fidelity_part), "dev")
    mine = lax.dynamic_slice_in_dim(summed_hist, position * per_device, per_device)
    amps_total = float(amps_local * devices)
    sample_probs = amps_total * (values / norm)
    histogram = float(bin_count) * (mine / norm)
    fidelity = amps_total * (total / norm) / float(samp_local * devices) - 1.0
    return (sample_probs, histogram, fidelity)


def solution(mesh):
    return jax.shard_map(
        shards,
        mesh=mesh,
        in_specs=(P(None, "dev"), P(), P("dev", None), P("dev"), P()),
        out_specs=(P("dev"), P("dev"), P()),
        check_vma=False,
    )
```

profile of v0, /device:TPU:0, one launch (start us, length us, event | category | flops | bytes accessed | tf_op | source)
XLA Modules:
  0.0 276.9 jit_solution(538801981134763704)
XLA Ops:
  15.6 7.5 %all-to-all-start.1 = ((f32[2,32,1024]{2,0,1:T(2,128)}), f32[2,32,1024]{2,0,1:T(2,128)S(1)}, u32[]{:S(2)}, u32[]{:S(2)}) async-start(f32[2,32,1024]{2,0,1:T(2,128)} %pad_maximum_fusion), calls=%async_computation.1 | async-start | bytes 524288 | tf_op jit(solution)/shard_map/all_to_all | solution.py:90
  26.3 15.3 %fusion.20 = s32[32,1,1024]{2,0,1:T(8,128)S(1)} fusion(f32[8192]{0:T(1024)S(1)} %bitcast.164, f32[8192]{0:T(1024)S(1)} %add_convert_fusion, s32[8192]{0:T(1024)S(1)} %bitcast.162), kind=kOutput, calls=%fused_computation.42 | convolution fusion | flops 3230203904 | bytes 229376 | tf_op jit(solution)/shard_map/dot_general | solution.py:126
  44.5 5.8 %all-to-all-start = ((s32[32,1,1024]{2,1,0:T(1,128)}), s32[32,1,1024]{2,1,0:T(1,128)S(1)}, u32[]{:S(2)}, u32[]{:S(2)}) async-start(s32[32,1,1024]{2,1,0:T(1,128)} %copy.42), calls=%async_computation | async-start | bytes 262144 | tf_op jit(solution)/shard_map/all_to_all | solution.py:130
  52.6 6.0 %all-to-all-done = s32[32,1,1024]{2,1,0:T(1,128)S(1)} async-done(((s32[32,1,1024]{2,1,0:T(1,128)}), s32[32,1,1024]{2,1,0:T(1,128)S(1)}, u32[]{:S(2)}, u32[]{:S(2)}) %all-to-all-start) | async-done | bytes 131104 | tf_op jit(solution)/shard_map/all_to_all | solution.py:130
  61.9 9.8 %all-to-all-done.2 = f32[2,32,1024]{2,0,1:T(2,128)S(1)} async-done(((f32[2,32,1024]{2,0,1:T(2,128)}), f32[2,32,1024]{2,0,1:T(2,128)S(1)}, u32[]{:S(2)}, u32[]{:S(2)}) %all-to-all-start.2) | async-done | bytes 262176 | tf_op jit(solution)/shard_map/all_to_all | solution.py:95
  72.6 112.7 %while.12 = (s32[]{:T(128)}, f32[32,1024]{1,0:T(8,128)S(1)}, s32[32,1024]{1,0:T(8,128)S(1)}, f32[256,128]{1,0:T(8,128)S(1)}) while((s32[]{:T(128)}, f32[32,1024]{1,0:T(8,128)S(1)}, s32[32,1024]{1,0:T(8,128)S(1)}, f32[256,128]{1,0:T(8,128)S(1)}) %tuple.101), condition=%wide.region_5.6_spmd.clone.clone, body=%wide.region_3.5_spmd.clone.sunk.clone | while | flops 535554 | bytes 1628233 | solution.py:64
  76.1 2.8 %gather_fusion = f32[1024,128]{1,0:T(8,128)S(1)} fusion(f32[256,128]{1,0:T(8,128)S(1)} %get-tuple-element.204, s32[1024]{0:T(1024)S(1)} %broadcast_clamp_fusion.4), kind=kCustom, calls=%fused_computation.clone.clone.1.clone | custom fusion | bytes 1052672 | tf_op jit(solution)/shard_map/while/body/eval_jaxpr/jit(_take)/gather | solution.py:59
  79.7 2.8 %gather_fusion = f32[1024,128]{1,0:T(8,128)S(1)} fusion(f32[256,128]{1,0:T(8,128)S(1)} %get-tuple-element.204, s32[1024]{0:T(1024)S(1)} %broadcast_clamp_fusion.4), kind=kCustom, calls=%fused_computation.clone.clone.1.clone | custom fusion | bytes 1052672 | tf_op jit(solution)/shard_map/while/body/eval_jaxpr/jit(_take)/gather | solution.py:59
  90.2 2.8 %gather_fusion = f32[1024,128]{1,0:T(8,128)S(1)} fusion(f32[256,128]{1,0:T(8,128)S(1)} %get-tuple-element.204, s32[1024]{0:T(1024)S(1)} %broadcast_clamp_fusion.4), kind=kCustom, calls=%fused_computation.clone.clone.1.clone | custom fusion | bytes 1052672 | tf_op jit(solution)/shard_map/while/body/eval_jaxpr/jit(_take)/gather | solution.py:59
  100.8 2.8 %gather_fusion = f32[1024,128]{1,0:T(8,128)S(1)} fusion(f32[256,128]{1,0:T(8,128)S(1)} %get-tuple-element.204, s32[1024]{0:T(1024)S(1)} %broadcast_clamp_fusion.4), kind=kCustom, calls=%fused_computation.clone.clone.1.clone | custom fusion | bytes 1052672 | tf_op jit(solution)/shard_map/while/body/eval_jaxpr/jit(_take)/gather | solution.py:59
  104.3 2.8 %gather_fusion = f32[1024,128]{1,0:T(8,128)S(1)} fusion(f32[256,128]{1,0:T(8,128)S(1)} %get-tuple-element.204, s32[1024]{0:T(1024)S(1)} %broadcast_clamp_fusion.4), kind=kCustom, calls=%fused_computation.clone.clone.1.clone | custom fusion | bytes 1052672 | tf_op jit(solution)/shard_map/while/body/eval_jaxpr/jit(_take)/gather | solution.py:59
  111.4 2.8 %gather_fusion = f32[1024,128]{1,0:T(8,128)S(1)} fusion(f32[256,128]{1,0:T(8,128)S(1)} %get-tuple-element.204, s32[1024]{0:T(1024)S(1)} %broadcast_clamp_fusion.4), kind=kCustom, calls=%fused_computation.clone.clone.1.clone | custom fusion | bytes 1052672 | tf_op jit(solution)/shard_map/while/body/eval_jaxpr/jit(_take)/gather | solution.py:59
  114.9 2.8 %gather_fusion = f32[1024,128]{1,0:T(8,128)S(1)} fusion(f32[256,128]{1,0:T(8,128)S(1)} %get-tuple-element.204, s32[1024]{0:T(1024)S(1)} %broadcast_clamp_fusion.4), kind=kCustom, calls=%fused_computation.clone.clone.1.clone | custom fusion | bytes 1052672 | tf_op jit(solution)/shard_map/while/body/eval_jaxpr/jit(_take)/gather | solution.py:59
  136.0 2.8 %gather_fusion = f32[1024,128]{1,0:T(8,128)S(1)} fusion(f32[256,128]{1,0:T(8,128)S(1)} %get-tuple-element.204, s32[1024]{0:T(1024)S(1)} %broadcast_clamp_fusion.4), kind=kCustom, calls=%fused_computation.clone.clone.1.clone | custom fusion | bytes 1052672 | tf_op jit(solution)/shard_map/while/body/eval_jaxpr/jit(_take)/gather | solution.py:59
  139.6 2.8 %gather_fusion = f32[1024,128]{1,0:T(8,128)S(1)} fusion(f32[256,128]{1,0:T(8,128)S(1)} %get-tuple-element.204, s32[1024]{0:T(1024)S(1)} %broadcast_clamp_fusion.4), kind=kCustom, calls=%fused_computation.clone.clone.1.clone | custom fusion | bytes 1052672 | tf_op jit(solution)/shard_map/while/body/eval_jaxpr/jit(_take)/gather | solution.py:59
  146.6 2.8 %gather_fusion = f32[1024,128]{1,0:T(8,128)S(1)} fusion(f32[256,128]{1,0:T(8,128)S(1)} %get-tuple-element.204, s32[1024]{0:T(1024)S(1)} %broadcast_clamp_fusion.4), kind=kCustom, calls=%fused_computation.clone.clone.1.clone | custom fusion | bytes 1052672 | tf_op jit(solution)/shard_map/while/body/eval_jaxpr/jit(_take)/gather | solution.py:59
  160.7 2.8 %gather_fusion = f32[1024,128]{1,0:T(8,128)S(1)} fusion(f32[256,128]{1,0:T(8,128)S(1)} %get-tuple-element.204, s32[1024]{0:T(1024)S(1)} %broadcast_clamp_fusion.4), kind=kCustom, calls=%fused_computation.clone.clone.1.clone | custom fusion | bytes 1052672 | tf_op jit(solution)/shard_map/while/body/eval_jaxpr/jit(_take)/gather | solution.py:59
  164.2 2.8 %gather_fusion = f32[1024,128]{1,0:T(8,128)S(1)} fusion(f32[256,128]{1,0:T(8,128)S(1)} %get-tuple-element.204, s32[1024]{0:T(1024)S(1)} %broadcast_clamp_fusion.4), kind=kCustom, calls=%fused_computation.clone.clone.1.clone | custom fusion | bytes 1052672 | tf_op jit(solution)/shard_map/while/body/eval_jaxpr/jit(_take)/gather | solution.py:59
  167.7 2.8 %gather_fusion = f32[1024,128]{1,0:T(8,128)S(1)} fusion(f32[256,128]{1,0:T(8,128)S(1)} %get-tuple-element.204, s32[1024]{0:T(1024)S(1)} %broadcast_clamp_fusion.4), kind=kCustom, calls=%fused_computation.clone.clone.1.clone | custom fusion | bytes 1052672 | tf_op jit(solution)/shard_map/while/body/eval_jaxpr/jit(_take)/gather | solution.py:59
  178.3 2.8 %gather_fusion = f32[1024,128]{1,0:T(8,128)S(1)} fusion(f32[256,128]{1,0:T(8,128)S(1)} %get-tuple-element.204, s32[1024]{0:T(1024)S(1)} %broadcast_clamp_fusion.4), kind=kCustom, calls=%fused_computation.clone.clone.1.clone | custom fusion | bytes 1052672 | tf_op jit(solution)/shard_map/while/body/eval_jaxpr/jit(_take)/gather | solution.py:59
  191.4 2.9 %copy.59 = f32[128,8,8,128]{3,1,2,0:T(8,128)} copy(f32[128,8,8,128]{3,2,1,0:T(8,128)S(1)} %convolution_bitcast_fusion) | data formatting | bytes 8388608
  194.3 15.2 %gather_fusion.1 = f32[1024]{0:T(1024)S(1)} fusion(f32[1048576]{0:T(1024)} %bitcast.157, s32[1024]{0:T(1024)S(1)} %broadcast_clamp_fusion.1), kind=kCustom, calls=%fused_computation.1 | custom fusion | bytes 12288 | tf_op jit(solution)/shard_map/jit(_take)/gather | solution.py:180
  210.2 20.9 %fusion.4 = (f32[]{:T(128)}, f32[8192]{0:T(1024)S(1)}) fusion(f32[8192]{0:T(1024)S(1)} %bitcast.165, f32[32,1,1024]{2,1,0:T(1,128)S(1)} %all-to-all-done.3, s32[8192]{0:T(1024)S(1)} %bitcast.163), kind=kOutput, calls=%fused_computation.14 | convolution fusion | flops 3255033856 | bytes 229380 | tf_op jit(solution)/shard_map/dot_general | solution.py:135
  231.1 40.7 %all-reduce.1 = (f32[]{:T(128)}, f32[1024]{0:T(1024)S(1)}, f32[]{:T(128)}) all-reduce(f32[]{:T(128)} %get-tuple-element.100, f32[1024]{0:T(1024)S(1)} %fusion.55, f32[]{:T(128)} %get-tuple-element.41), channel_id=1, replica_groups=mesh['dev'=32] {'dev'}, use_global_device_ids=true, to_apply=%region_8.9 | all-reduce | flops 1026 | bytes 8208 | tf_op jit(solution)/shard_map/psum | solution.py:103
  (337 shorter events, 107.7 us)
Async XLA Ops:
  3.2 3.6 %copy-start = (f32[2,32768]{1,0:T(2,128)S(1)}, f32[2,32768]{1,0:T(2,128)}, u32[]{:S(2)}) copy-start(f32[2,32768]{1,0:T(2,128)} %param.7) | copy-start | bytes 786436
  10.2 13.7 %copy-start.2 = (s32[8192,1]{0,1:T(1,128)S(1)}, s32[8192,1]{0,1:T(1,128)}, u32[]{:S(2)}) copy-start(s32[8192,1]{0,1:T(1,128)} %param.9) | copy-start | bytes 98308
  11.9 13.7 %copy-start.1 = (s32[8192]{0:T(1024)S(1)}, s32[8192]{0:T(1024)}, u32[]{:S(2)}) copy-start(s32[8192]{0:T(1024)} %param.10) | copy-start | bytes 98308
  12.0 14.3 %copy-start.3 = (s32[10]{0:T(128)S(1)}, s32[10]{0:T(128)}, u32[]{:S(2)}) copy-start(s32[10]{0:T(128)} %param.11) | copy-start | bytes 124
  15.6 28.9 %all-to-all-start.1 = ((f32[2,32,1024]{2,0,1:T(2,128)}), f32[2,32,1024]{2,0,1:T(2,128)S(1)}, u32[]{:S(2)}, u32[]{:S(2)}) async-start(f32[2,32,1024]{2,0,1:T(2,128)} %pad_maximum_fusion), calls=%async_computation.1 | async-start | bytes 524288 | tf_op jit(solution)/shard_map/all_to_all | solution.py:90
  44.5 14.1 %all-to-all-start = ((s32[32,1,1024]{2,1,0:T(1,128)}), s32[32,1,1024]{2,1,0:T(1,128)S(1)}, u32[]{:S(2)}, u32[]{:S(2)}) async-start(s32[32,1,1024]{2,1,0:T(1,128)} %copy.42), calls=%async_computation | async-start | bytes 262144 | tf_op jit(solution)/shard_map/all_to_all | solution.py:130
  58.6 13.1 %all-to-all-start.2 = ((f32[2,32,1024]{2,0,1:T(2,128)}), f32[2,32,1024]{2,0,1:T(2,128)S(1)}, u32[]{:S(2)}, u32[]{:S(2)}) async-start(f32[2,32,1024]{2,0,1:T(2,128)} %copy.53), calls=%async_computation.2 | async-start | bytes 524288 | tf_op jit(solution)/shard_map/all_to_all | solution.py:95
  186.2 24.1 %all-to-all-start.3 = ((f32[32,1,1024]{2,1,0:T(1,128)}), f32[32,1,1024]{2,1,0:T(1,128)S(1)}, u32[]{:S(2)}, u32[]{:S(2)}) async-start(f32[32,1,1024]{2,1,0:T(1,128)} %copy.54), calls=%async_computation.3 | async-start | bytes 262144 | tf_op jit(solution)/shard_map/all_to_all | solution.py:133
where the time goes:
time: 276 us; the launch traced here: 277 us
  local copies, waits for them, and re-layouts  122 us (44%)
  matrix products  44.5 us (16%)
  blocking collectives  40.7 us (15%)
  other arithmetic  29.6 us (11%)
  starting transfers between devices  18.5 us (7%)
  waiting for transfers between devices  15.8 us (6%)
  between operations  3.69 us (1%)
    gather x32, local copies, waits for them, and re-layouts, one_block(): picked = jnp.take(weight_rows, upper, axis=0)  89.9 us
    psum x1, blocking collectives, shards(): norm = lax.psum(jnp.sum(weight), 'dev')  40.7 us
    dot_general x1, matrix products, shards(): jnp.dot(owner_hot, replies, precision=lax.Precision.HIGHEST) * rank_hot  20.9 us
    reduce_sum x32, other arithmetic, one_block(): jnp.sum(jnp.where(lower[:, None] == lane_ids[None, :], picked, 0.0), axis=1)  15.9 us
    dot_general x1, matrix products, shards(): jnp.dot((owner_hot * shifted_low[:, None]).T, rank_hot, precision=lax.Pre...  15.3 us
    gather x1, local copies, waits for them, and re-layouts, shards(): jnp.take(joint.reshape(bin_count * bin_count), line_ids * bin_count + col...  15.2 us
    all_to_all x1, waiting for transfers between devices, shards(): lax.all_to_all(jnp.stack([new_real[0], new_imag[0]]), 'dev', split_axis=1...  9.81 us
    all_to_all x1, starting transfers between devices, shards(): lax.all_to_all(stacked, 'dev', split_axis=1, concat_axis=1, tiled=True)  7.54 us
  transfers between devices with their start and end apart: 4, of which 2 were waited for; matrix products, arithmetic and copies ran while one was open for 16% of the time, Pallas kernels for 0%

commit v1 on v0

v1 whole, which is shorter than its diff:
```python
import functools

import jax
import jax.numpy as jnp
from jax import lax
from jax.experimental import pallas as pl
from jax.experimental.pallas import tpu as pltpu
from jax.sharding import PartitionSpec as P

LANES = 128
SUBLANES = 8
f32 = jnp.float32
bf16 = jnp.bfloat16
i32 = jnp.int32


def gate_table(angles):
    entry = jnp.arange(8, dtype=i32)[None, :]
    cell = entry >> 1
    theta, first, second = angles[:, 0:1], angles[:, 1:2], angles[:, 2:3]
    phase = jnp.where(cell >= 2, first, 0.0) + jnp.where((cell & 1) == 1, second, 0.0)
    size = jnp.where((cell == 0) | (cell == 3), jnp.cos(theta), jnp.sin(theta))
    turn = jnp.where((entry & 1) == 0, jnp.cos(phase), jnp.sin(phase))
    return jnp.where(cell == 1, -1.0, 1.0) * size * turn


def iota(shape, dim):
    return lax.broadcasted_iota(i32, shape, dim)


def leading_gate(xr, xi, bit, u):
    n, s, lanes = xr.shape
    shape = (n >> (bit + 1), 2, 1 << bit, s, lanes)
    xr, xi = xr.reshape(shape), xi.reshape(shape)
    ar, ai, br, bi = xr[:, 0], xi[:, 0], xr[:, 1], xi[:, 1]
    outs_r, outs_i = [], []
    for row in range(2):
        pr, pi, qr, qi = u[4 * row : 4 * row + 4]
        outs_r.append(pr * ar - pi * ai + (qr * br - qi * bi))
        outs_i.append(pr * ai + pi * ar + (qr * bi + qi * br))
    return (
        jnp.stack(outs_r, 1).reshape(n, s, lanes),
        jnp.stack(outs_i, 1).reshape(n, s, lanes),
    )


def sublane_gate(xr, xi, bit, u):
    step = 1 << bit
    high = ((iota((SUBLANES, LANES), 0) >> bit) & 1) == 1

    def swap(x):
        down = pltpu.roll(x, step, 1)
        if 2 * step == SUBLANES:
            return down
        return jnp.where(high[None], down, pltpu.roll(x, SUBLANES - step, 1))

    keep_r = jnp.where(high, u[6], u[0])[None]
    keep_i = jnp.where(high, u[7], u[1])[None]
    cross_r = jnp.where(high, u[4], u[2])[None]
    cross_i = jnp.where(high, u[5], u[3])[None]
    yr, yi = swap(xr), swap(xi)
    return (
        keep_r * xr - keep_i * xi + (cross_r * yr - cross_i * yi),
        keep_r * xi + keep_i * xr + (cross_r * yi + cross_i * yr),
    )


def lane_matrix(units):
    shape = (LANES, LANES)
    row, col = iota(shape, 0), iota(shape, 1)
    mr = mi = None
    for bit, u in enumerate(units):
        rb, cb = ((row >> bit) & 1) == 1, ((col >> bit) & 1) == 1
        gr = jnp.where(cb, jnp.where(rb, u[6], u[4]), jnp.where(rb, u[2], u[0]))
        gi = jnp.where(cb, jnp.where(rb, u[7], u[5]), jnp.where(rb, u[3], u[1]))
        if mr is None:
            mr, mi = gr, gi
        else:
            mr, mi = mr * gr - mi * gi, mr * gi + mi * gr
    return mr, mi


def cut(x, depth):
    rows = x.shape[0]
    x = x.reshape(rows // SUBLANES, SUBLANES, LANES)
    per = SUBLANES // depth
    if per == 1:
        return x
    parts = [x[:, k * depth : (k + 1) * depth] for k in range(per)]
    return jnp.stack(parts, 1).reshape(rows // depth, depth, LANES)


def join(x):
    n, depth, _ = x.shape
    per = SUBLANES // depth
    if per > 1:
        x = x.reshape(n // per, per, depth, LANES)
        x = jnp.concatenate([x[:, k] for k in range(per)], axis=1)
    return x.reshape(n * depth, LANES)


def halves(x):
    top = x.astype(bf16)
    return top, (x - top.astype(f32)).astype(bf16)


def one_hot(row, count):
    wide = jnp.broadcast_to(row.astype(f32), (16, LANES)).astype(bf16)
    ids = iota((count, LANES), 0).astype(f32).astype(bf16).reshape(count // 16, 16, LANES)
    hot = jnp.where(ids == wide[None], jnp.ones((), bf16), jnp.zeros((), bf16))
    return hot.reshape(count, LANES)


def split_table(table):
    flipped = table.T
    top, rest = halves(flipped)
    return jnp.concatenate([top, rest], axis=0)


def lookup(table, upper, lower):
    rows = upper.shape[0]
    count = table.shape[1]
    hot = jnp.concatenate([one_hot(upper[r : r + 1], count) for r in range(rows)], axis=1)
    both = jnp.dot(table, hot, preferred_element_type=f32)
    lane_ids = iota((LANES, LANES), 0)
    found = []
    for r in range(rows):
        part = slice(r * LANES, (r + 1) * LANES)
        value = both[:LANES, part] + both[LANES:, part]
        value = jnp.where(lane_ids == lower[r : r + 1], value, 0.0)
        found.append(jnp.sum(value, axis=0, keepdims=True))
    return jnp.concatenate(found, axis=0)


def kernel(
    sizes,
    gates,
    marg,
    state,
    owner_ref,
    low_ref,
    probs_ref,
    hist_ref,
    fid_ref,
    amp_out,
    amp_in,
    wt_out,
    wt_in,
    req_out,
    req_in,
    ans_out,
    ans_in,
    his_out,
    his_in,
    tot_out,
    tot_in,
    code_ref,
    rank_ref,
    table_ref,
    sends,
    recvs,
):
    devices, depth, capacity_rows, marg_count, amps_total, samples = sizes
    me = lax.axis_index("dev")
    global_bits = devices.bit_length() - 1
    rows = state.shape[1]
    row_bits = rows.bit_length() - 1
    local_bits = row_bits + 7
    codes = devices * capacity_rows

    def peer(k):
        return lax.rem(me + k, devices)

    def copy(channel, src, dst, target):
        return pltpu.make_async_remote_copy(
            src_ref=src,
            dst_ref=dst,
            send_sem=sends.at[channel],
            recv_sem=recvs.at[channel],
            device_id=(target,),
            device_id_type=pl.DeviceIdType.MESH,
        )

    def scatter(channel, out, into):
        @pl.loop(1, devices)
        def _(k):
            target = peer(k)
            copy(channel, out.at[target], into.at[me], target).start()

        into[me] = out[me]

    def spread(channel, out, into):
        @pl.loop(1, devices)
        def _(k):
            copy(channel, out.at[0], into.at[me], peer(k)).start()

        into[me] = out[0]

    def all_of(channel, into):
        many = into.at[pl.ds(0, devices - 1)]
        return copy(channel, many, many, peer(1))

    barrier = pltpu.get_barrier_semaphore()

    @pl.loop(1, devices)
    def _(k):
        pl.semaphore_signal(
            barrier, inc=1, device_id=(peer(k),), device_id_type=pl.DeviceIdType.MESH
        )

    def unit(qubit):
        return [gates[qubit, e] for e in range(8)]

    mr, mi = lane_matrix([unit(q) for q in range(7)])
    mixed = jnp.concatenate(
        [jnp.concatenate([mr, mi], axis=1), jnp.concatenate([-mi, mr], axis=1)], axis=0
    )
    both = jnp.concatenate([state[0], state[1]], axis=1)
    both = jnp.dot(both, mixed, precision=lax.Precision.HIGHEST, preferred_element_type=f32)
    xr = both[:, :LANES].reshape(rows // SUBLANES, SUBLANES, LANES)
    xi = both[:, LANES:].reshape(rows // SUBLANES, SUBLANES, LANES)
    for bit in range(3):
        xr, xi = sublane_gate(xr, xi, bit, unit(7 + bit))
    for bit in range(row_bits - 3):
        xr, xi = leading_gate(xr, xi, bit, unit(10 + bit))
    amp_out[:, 0] = cut(xr.reshape(rows, LANES), depth)
    amp_out[:, 1] = cut(xi.reshape(rows, LANES), depth)

    pl.semaphore_wait(barrier, devices - 1)
    scatter(0, amp_out, amp_in)

    samp_rows = owner_ref.shape[0]
    owner = owner_ref[...]
    owner_ids = iota((devices, LANES), 0)
    chunks = samp_rows // 2
    hot_rows = [(owner_ids == owner[r : r + 1]) for r in range(samp_rows)]
    pieces = [h.astype(f32).astype(bf16) for h in hot_rows]
    stacked = jnp.concatenate(
        [jnp.concatenate(pieces[2 * c : 2 * c + 2], axis=1) for c in range(chunks)], axis=0
    )
    tri_shape = (2 * LANES, 3 * LANES)
    tri_row, tri_col = iota(tri_shape, 0), iota(tri_shape, 1)
    tri = ((tri_row < tri_col) | (tri_col >= 2 * LANES)).astype(f32).astype(bf16)
    counts = jnp.dot(stacked, tri, preferred_element_type=f32)
    before = jnp.zeros((devices, LANES), f32)
    ranks = []
    for c in range(chunks):
        block = counts[c * devices : (c + 1) * devices]
        for h in range(2):
            spot = block[:, h * LANES : (h + 1) * LANES] + before
            mine = owner_ids == owner[2 * c + h : 2 * c + h + 1]
            ranks.append(jnp.sum(jnp.where(mine, spot, 0.0), axis=0, keepdims=True))
        before = before + block[:, 2 * LANES :]
    ranking = jnp.concatenate(ranks, axis=0).astype(i32)
    code_ref[...] = owner * capacity_rows + (ranking >> 7)
    rank_ref[...] = ranking & (LANES - 1)

    lane_ids = iota((LANES, LANES), 0)
    steps = samp_rows // SUBLANES

    def place(t, placed):
        window = pl.ds(pl.multiple_of(t * SUBLANES, SUBLANES), SUBLANES)
        code, rank, low = code_ref[window], rank_ref[window], low_ref[window] + 1
        low_top = (low >> 8).astype(f32)
        low_rest = (low & 255).astype(f32)
        hot = jnp.concatenate([one_hot(code[r : r + 1], codes) for r in range(SUBLANES)], axis=1)
        tops, rests = [], []
        for r in range(SUBLANES):
            here = lane_ids == rank[r : r + 1]
            tops.append(jnp.where(here, low_top[r : r + 1], 0.0).astype(bf16))
            rests.append(jnp.where(here, low_rest[r : r + 1], 0.0).astype(bf16))
        values = jnp.concatenate(
            [jnp.concatenate(tops, axis=1), jnp.concatenate(rests, axis=1)], axis=0
        )
        return placed + lax.dot_general(
            hot, values, (((1,), (1,)), ((), ())), preferred_element_type=f32
        )

    placed = lax.fori_loop(0, steps, place, jnp.zeros((codes, 2 * LANES), f32))
    wanted = (placed[:, :LANES] * 256.0 + placed[:, LANES:]).astype(i32) - 1
    req_out[...] = cut(wanted, capacity_rows)
    scatter(1, req_out, req_in)

    all_of(0, amp_in).wait_recv()
    xr, xi = amp_in[:, 0], amp_in[:, 1]
    for bit in range(global_bits):
        xr, xi = leading_gate(xr, xi, bit, unit(local_bits + bit))
    weight = xr * xr + xi * xi
    wt_out[...] = weight
    scatter(2, wt_out, wt_in)

    weight = join(weight)
    norm_part = jnp.sum(weight, axis=0, keepdims=True)
    low_depth = depth.bit_length() - 1
    code_shape = (rows, LANES)
    row_id = iota(code_shape, 0)
    row_value = (
        ((row_id >> low_depth) << local_bits)
        + (me << (7 + low_depth))
        + ((row_id & (depth - 1)) << 7)
    )
    lane_value = iota((LANES, LANES), 0)
    row_code = jnp.zeros(code_shape, i32)
    lane_code = jnp.zeros((LANES, LANES), i32)
    lane_mask = jnp.zeros((), i32)
    for k in range(marg_count):
        qubit = marg[0, k]
        row_code = row_code + (((row_value >> qubit) & 1) << k)
        lane_code = lane_code + (((lane_value >> qubit) & 1) << k)
        lane_mask = lane_mask + jnp.where(qubit < 7, 1 << k, 0)
    bins = 2**marg_count
    top, rest = halves(weight)
    split = jnp.concatenate([top, rest], axis=0)
    @pl.loop(0, bins // LANES)
    def _(c):
        bin_id = c * LANES + iota((1, LANES), 1)
        lane_part = bin_id & lane_mask
        lane_hot = (lane_code == lane_part).astype(f32).astype(bf16)
        folded = jnp.dot(split, lane_hot, preferred_element_type=f32)
        folded = folded[:rows] + folded[rows:]
        picked = jnp.where(row_code == bin_id - lane_part, folded, 0.0)
        his_out[0, pl.ds(c, 1)] = jnp.sum(picked, axis=0, keepdims=True)

    spread(4, his_out, his_in)

    all_of(1, req_in).wait_recv()
    all_of(2, wt_in).wait_recv()
    table_ref[...] = split_table(join(wt_in[...]))

    def answer(target):
        wanted = req_in[target]
        return lookup(table_ref[...], wanted >> 7, wanted & (LANES - 1))

    def reply(k, total):
        target = peer(k)
        found = answer(target)
        ans_out[target] = found
        copy(3, ans_out.at[target], ans_in.at[me], target).start()
        return total + jnp.sum(found, axis=0, keepdims=True)

    total = lax.fori_loop(1, devices, reply, jnp.zeros((1, LANES), f32))
    found = answer(me)
    ans_in[me] = found
    total = total + jnp.sum(found, axis=0, keepdims=True)
    tot_out[0, 0:1] = total
    tot_out[0, 1:2] = norm_part
    spread(5, tot_out, tot_in)

    all_of(3, ans_in).wait_recv()
    table_ref[...] = split_table(join(ans_in[...]))

    def fetch(t, carry):
        window = pl.ds(pl.multiple_of(t * SUBLANES, SUBLANES), SUBLANES)
        probs_ref[window] = lookup(table_ref[...], code_ref[window], rank_ref[window])
        return carry

    lax.fori_loop(0, steps, fetch, 0)
    all_of(5, tot_in).wait_recv()
    all_of(4, his_in).wait_recv()
    sums = jnp.sum(jnp.sum(tot_in[...], axis=0), axis=1, keepdims=True)
    total, norm = sums[0:1], sums[1:2]
    probs_ref[...] = amps_total * (probs_ref[...] / norm)
    hist_ref[...] = float(bins) * (jnp.sum(his_in[...], axis=0) / norm)
    fid = amps_total * (total / norm) / samples - 1.0
    fid_ref[...] = jnp.broadcast_to(fid, (1, LANES))

    for channel, into in enumerate((amp_in, req_in, wt_in, ans_in, his_in, tot_in)):
        all_of(channel, into).wait_send()


def shards(state, angles, sample_high, sample_low, marginal_qubits):
    devices = lax.axis_size("dev")
    position = lax.axis_index("dev")
    amps_local = state.shape[1]
    samp_local = sample_low.shape[0]
    marg_count = marginal_qubits.shape[0]
    bins = 2**marg_count
    depth = amps_local // devices // LANES
    capacity_rows = 4 * samp_local // devices // LANES
    rows = amps_local // LANES
    samp_rows = samp_local // LANES
    sizes = (
        devices,
        depth,
        capacity_rows,
        marg_count,
        float(amps_local * devices),
        float(samp_local * devices),
    )
    vmem = pl.BlockSpec(memory_space=pltpu.VMEM)
    smem = pl.BlockSpec(memory_space=pltpu.SMEM)
    codes = devices * capacity_rows
    bin_rows = bins // LANES
    probs, hist, fid = pl.pallas_call(
        functools.partial(kernel, sizes),
        out_shape=(
            jax.ShapeDtypeStruct((samp_rows, LANES), f32),
            jax.ShapeDtypeStruct((bin_rows, LANES), f32),
            jax.ShapeDtypeStruct((1, LANES), f32),
        ),
        in_specs=[smem, smem, vmem, vmem, vmem],
        out_specs=(vmem, vmem, vmem),
        scratch_shapes=[
            pltpu.VMEM((devices, 2, depth, LANES), f32),
            pltpu.VMEM((devices, 2, depth, LANES), f32),
            pltpu.VMEM((devices, depth, LANES), f32),
            pltpu.VMEM((devices, depth, LANES), f32),
            pltpu.VMEM((devices, capacity_rows, LANES), i32),
            pltpu.VMEM((devices, capacity_rows, LANES), i32),
            pltpu.VMEM((devices, capacity_rows, LANES), f32),
            pltpu.VMEM((devices, capacity_rows, LANES), f32),
            pltpu.VMEM((1, bin_rows, LANES), f32),
            pltpu.VMEM((devices, bin_rows, LANES), f32),
            pltpu.VMEM((1, 2, LANES), f32),
            pltpu.VMEM((devices, 2, LANES), f32),
            pltpu.VMEM((samp_rows, LANES), i32),
            pltpu.VMEM((samp_rows, LANES), i32),
            pltpu.VMEM((2 * LANES, max(rows, codes)), bf16),
            pltpu.SemaphoreType.DMA((6,)),
            pltpu.SemaphoreType.DMA((6,)),
        ],
        compiler_params=pltpu.CompilerParams(collective_id=0, has_side_effects=True),
        name="circuit",
    )(
        gate_table(angles),
        marginal_qubits.reshape(1, marg_count),
        state.reshape(2, rows, LANES),
        sample_high.reshape(samp_rows, LANES),
        sample_low.reshape(samp_rows, LANES),
    )
    per_device = bins // devices
    mine = lax.dynamic_slice_in_dim(hist.reshape(bins), position * per_device, per_device)
    return probs.reshape(samp_local), mine, fid[0, 0]


def solution(mesh):
    return jax.shard_map(
        shards,
        mesh=mesh,
        in_specs=(P(None, "dev"), P(), P("dev", None), P("dev"), P()),
        out_specs=(P("dev"), P("dev"), P()),
        check_vma=False,
    )
```

time: 276 us -> 48.5 us (0.18)
  local copies, waits for them, and re-layouts: 122 us -> 5.14 us
  matrix products: 44.5 us -> 0 us
  blocking collectives: 40.7 us -> 0 us
  Pallas kernels: 0 us -> 40.5 us
  other arithmetic: 29.6 us -> 0.75 us
  starting transfers between devices: 18.5 us -> 0 us
  waiting for transfers between devices: 15.8 us -> 0 us
    gather x33 -> x0, local copies, waits for them, and re-layouts: 105 us -> none  [the longest x32 89.9 us: one_block(): picked = jnp.take(weight_rows, upper, axis=0)]
    dot_general x21 -> x0, matrix products: 44.5 us -> none  [the longest x1 20.9 us: shards(): jnp.dot(owner_hot, replies, precision=lax.Precision.HIGHEST) * rank_hot]
    psum x1 -> x0, blocking collectives: 40.7 us -> none  [shards(): norm = lax.psum(jnp.sum(weight), 'dev')]
    pallas_call x0 -> x1, Pallas kernels: none -> 40.5 us  [shards(): pl.pallas_call(functools.partial(kernel, sizes), out_shape=(jax.ShapeDtyp...]
    all_to_all x4 -> x0, starting transfers between devices: 18.5 us -> none  [the longest x1 7.54 us: shards(): lax.all_to_all(stacked, 'dev', split_axis=1, concat_axis=1, tiled=True)]
    reduce_sum x37 -> x0, other arithmetic: 17.8 us -> none  [the longest x32 15.9 us: one_block(): jnp.sum(jnp.where(lower[:, None] == lane_ids[None, :], picked, 0.0), axis=1)]
    all_to_all x4 -> x0, waiting for transfers between devices: 15.8 us -> none  [the longest x1 9.81 us: shards(): lax.all_to_all(jnp.stack([new_real[0], new_imag[0]]), 'dev', split_axis=1...]
    dynamic_update_slice x32 -> x0, local copies, waits for them, and re-layouts: 3.52 us -> none  [lookup_rows(): lax.map(one_block, offsets.reshape(total // 1024, 1024)).reshape(total)]
  transfers between devices with their start and end apart: 4 -> 0, of which waited for: 2 -> 0; matrix products, arithmetic and copies ran while one was open for 16% -> 0% of each run, Pallas kernels for 0% -> 0%
where the time goes in v1:
time: 48.5 us; the launch traced here: 48.2 us
  Pallas kernels  40.5 us (84%)
  local copies, waits for them, and re-layouts  5.14 us (11%)
  between operations  1.83 us (4%)
  other arithmetic  0.75 us (2%)
    pallas_call x1, Pallas kernels, shards(): pl.pallas_call(functools.partial(kernel, sizes), out_shape=(jax.ShapeDtyp...  40.5 us
    unnamed x4, local copies, waits for them, and re-layouts  3.04 us
    dynamic_slice x1, local copies, waits for them, and re-layouts, shards(): lax.dynamic_slice_in_dim(hist.reshape(bins), position * per_device, per_d...  1.27 us

profile of v1, /device:TPU:0, one launch (start us, length us, event | category | flops | bytes accessed | tf_op | source)
XLA Modules:
  0.0 48.2 jit_solution(12583494910828066328)
XLA Ops:
  0.6 0.8 %cosine_bitcast_fusion = (f32[20]{0:T(128)S(1)}, f32[20]{0:T(128)S(1)}, f32[20]{0:T(128)S(1)}, f32[20]{0:T(128)S(1)}) fusion(f32[20,3]{0,1:T(4,128)} %param.6), kind=kLoop, calls=%fused_computation.9 | loop fusion | bytes 560 | tf_op jit(solution)/shard_map/jit(_where)/broadcast_in_dim | solution.py:22
  1.5 0.7 %select_multiply_fusion.gates = f32[20,8]{1,0:T(8,128)} fusion(f32[20]{0:T(128)S(1)} %get-tuple-element.11, f32[20]{0:T(128)S(1)} %get-tuple-element.12, f32[20]{0:T(128)S(1)} %get-tuple-element.10, f32[20]{0:T(128)S(1)} %get-tuple-element.9, f32[8]{0:T(128)S(1)} %compare_select_fusion, pred[8]{0:T(512)(128)(4,1)S(1)} %get-tuple-element.14, ...), kind=kLoop, calls=%fused_computation.1 | loop fusion | flops 1120 | bytes 1024 | tf_op jit(solution)/shard_map/mul | solution.py:24
  2.2 1.7 %copy.10 = f32[1,2,256,128]{3,2,1,0:T(8,128)} copy(f32[1,2,256,128]{3,1,2,0:T(2,128)} %bitcast.20) | data formatting | bytes 524288
  3.9 40.5 %circuit.1 = (f32[64,128]{1,0:T(8,128)}, f32[8,128]{1,0:T(8,128)}, f32[1,128]{1,0:T(1,128)}) custom-call(f32[20,8]{1,0:T(8,128)} %select_multiply_fusion.gates, s32[1,10]{1,0:T(1,128)} %bitcast.24, f32[2,256,128]{2,1,0:T(8,128)} %bitcast.19, s32[64,128]{1,0:T(8,128)} %bitcast.22, s32[64,128]{1,0:T(8,128)} %bitcast.23), custom_call_target="tpu_custom_call" | custom-call | tf_op jit(solution)/shard_map/circuit/pallas_call | solution.py:394
  44.4 1.3 %dynamic_slice.3 = f32[32]{0:T(128)} dynamic-slice(f32[1024]{0:T(1024)} %bitcast.25, s32[]{:T(128)S(6)} %select_n.32), dynamic_slice_sizes={32} | dynamic-slice | bytes 260 | tf_op jit(solution)/shard_map/dynamic_slice | solution.py:432
  45.6 0.0 copy-start
  45.6 1.4 %copy.13 = f32[8192]{0:T(1024)} copy(f32[8192]{0:T(1024)} %bitcast.21) | data formatting | bytes 65536
  47.0 0.0 copy-done
  (3 shorter events, 0.0 us)
Async XLA Ops:
  45.6 1.4 %copy-start = (f32[1,128]{1,0:T(1,128)S(1)}, f32[1,128]{1,0:T(1,128)}, u32[]{:S(2)}) copy-start(f32[1,128]{1,0:T(1,128)} %get-tuple-element.8) | copy-start | bytes 1540

commit v2 on v1

--- a/solution.py
+++ b/solution.py
@@ -14,18 +14,35 @@
 i32 = jnp.int32
 
 
-def gate_table(angles):
-    entry = jnp.arange(8, dtype=i32)[None, :]
-    cell = entry >> 1
-    theta, first, second = angles[:, 0:1], angles[:, 1:2], angles[:, 2:3]
-    phase = jnp.where(cell >= 2, first, 0.0) + jnp.where((cell & 1) == 1, second, 0.0)
-    size = jnp.where((cell == 0) | (cell == 3), jnp.cos(theta), jnp.sin(theta))
-    turn = jnp.where((entry & 1) == 0, jnp.cos(phase), jnp.sin(phase))
-    return jnp.where(cell == 1, -1.0, 1.0) * size * turn
-
-
 def iota(shape, dim):
     return lax.broadcasted_iota(i32, shape, dim)
+
+
+def gate_rows(angles, qubits):
+    sub = iota((SUBLANES, LANES), 0)
+
+    def column(j):
+        blocks = []
+        for first in range(0, qubits, SUBLANES):
+            block = jnp.zeros((SUBLANES, LANES), f32)
+            for q in range(first, min(first + SUBLANES, qubits)):
+                block = jnp.where(sub == q - first, angles[j, q], block)
+            blocks.append(block)
+        return jnp.concatenate(blocks, axis=0)
+
+    theta, first, second = column(0), column(1), column(2)
+    cosine, sine = jnp.cos(theta), jnp.sin(theta)
+    joint = first + second
+    return [
+        cosine,
+        jnp.zeros_like(cosine),
+        -jnp.cos(second) * sine,
+        -jnp.sin(second) * sine,
+        jnp.cos(first) * sine,
+        jnp.sin(first) * sine,
+        jnp.cos(joint) * cosine,
+        jnp.sin(joint) * cosine,
+    ]
 
 
 def leading_gate(xr, xi, bit, u):
@@ -134,7 +151,7 @@
 
 def kernel(
     sizes,
-    gates,
+    angles,
     marg,
     state,
     owner_ref,
@@ -157,13 +174,15 @@
     code_ref,
     rank_ref,
     table_ref,
+    gates,
     sends,
     recvs,
+    req_recvs,
 ):
     devices, depth, capacity_rows, marg_count, amps_total, samples = sizes
     me = lax.axis_index("dev")
     global_bits = devices.bit_length() - 1
-    rows = state.shape[1]
+    rows = state.shape[0] // 2
     row_bits = rows.bit_length() - 1
     local_bits = row_bits + 7
     codes = devices * capacity_rows
@@ -200,6 +219,16 @@
         many = into.at[pl.ds(0, devices - 1)]
         return copy(channel, many, many, peer(1))
 
+    def ask(src, source, target):
+        return pltpu.make_async_remote_copy(
+            src_ref=src,
+            dst_ref=req_in.at[source],
+            send_sem=sends.at[1],
+            recv_sem=req_recvs.at[source],
+            device_id=(target,),
+            device_id_type=pl.DeviceIdType.MESH,
+        )
+
     barrier = pltpu.get_barrier_semaphore()
 
     @pl.loop(1, devices)
@@ -208,14 +237,19 @@
             barrier, inc=1, device_id=(peer(k),), device_id_type=pl.DeviceIdType.MESH
         )
 
+    for e, entry in enumerate(gate_rows(angles, global_bits + local_bits)):
+        gates[e] = entry
+
     def unit(qubit):
-        return [gates[qubit, e] for e in range(8)]
+        return [gates[e, qubit : qubit + 1] for e in range(8)]
 
     mr, mi = lane_matrix([unit(q) for q in range(7)])
     mixed = jnp.concatenate(
         [jnp.concatenate([mr, mi], axis=1), jnp.concatenate([-mi, mr], axis=1)], axis=0
     )
-    both = jnp.concatenate([state[0], state[1]], axis=1)
+    both = jnp.concatenate(
+        [state[pl.ds(0, rows, stride=2)], state[pl.ds(1, rows, stride=2)]], axis=1
+    )
     both = jnp.dot(both, mixed, precision=lax.Precision.HIGHEST, preferred_element_type=f32)
     xr = both[:, :LANES].reshape(rows // SUBLANES, SUBLANES, LANES)
     xi = both[:, LANES:].reshape(rows // SUBLANES, SUBLANES, LANES)
@@ -279,7 +313,6 @@
     placed = lax.fori_loop(0, steps, place, jnp.zeros((codes, 2 * LANES), f32))
     wanted = (placed[:, :LANES] * 256.0 + placed[:, LANES:]).astype(i32) - 1
     req_out[...] = cut(wanted, capacity_rows)
-    scatter(1, req_out, req_in)
 
     all_of(0, amp_in).wait_recv()
     xr, xi = amp_in[:, 0], amp_in[:, 1]
@@ -288,6 +321,11 @@
     weight = xr * xr + xi * xi
     wt_out[...] = weight
     scatter(2, wt_out, wt_in)
+
+    @pl.loop(1, devices)
+    def _(k):
+        target = peer(k)
+        ask(req_out.at[target], me, target).start()
 
     weight = join(weight)
     norm_part = jnp.sum(weight, axis=0, keepdims=True)
@@ -321,27 +359,26 @@
         picked = jnp.where(row_code == bin_id - lane_part, folded, 0.0)
         his_out[0, pl.ds(c, 1)] = jnp.sum(picked, axis=0, keepdims=True)
 
+
+    all_of(2, wt_in).wait_recv()
     spread(4, his_out, his_in)
-
-    all_of(1, req_in).wait_recv()
-    all_of(2, wt_in).wait_recv()
     table_ref[...] = split_table(join(wt_in[...]))
 
-    def answer(target):
-        wanted = req_in[target]
+    def answer(wanted):
         return lookup(table_ref[...], wanted >> 7, wanted & (LANES - 1))
 
+    found = answer(req_out[me])
+    ans_in[me] = found
+
     def reply(k, total):
-        target = peer(k)
-        found = answer(target)
-        ans_out[target] = found
-        copy(3, ans_out.at[target], ans_in.at[me], target).start()
+        source = peer(devices - k)
+        ask(req_out.at[source], source, source).wait_recv()
+        found = answer(req_in[source])
+        ans_out[source] = found
+        copy(3, ans_out.at[source], ans_in.at[me], source).start()
         return total + jnp.sum(found, axis=0, keepdims=True)
 
-    total = lax.fori_loop(1, devices, reply, jnp.zeros((1, LANES), f32))
-    found = answer(me)
-    ans_in[me] = found
-    total = total + jnp.sum(found, axis=0, keepdims=True)
+    total = lax.fori_loop(1, devices, reply, jnp.sum(found, axis=0, keepdims=True))
     tot_out[0, 0:1] = total
     tot_out[0, 1:2] = norm_part
     spread(5, tot_out, tot_in)
@@ -416,15 +453,17 @@
             pltpu.VMEM((samp_rows, LANES), i32),
             pltpu.VMEM((samp_rows, LANES), i32),
             pltpu.VMEM((2 * LANES, max(rows, codes)), bf16),
+            pltpu.VMEM((8, -(-angles.shape[0] // SUBLANES) * SUBLANES, LANES), f32),
             pltpu.SemaphoreType.DMA((6,)),
             pltpu.SemaphoreType.DMA((6,)),
+            pltpu.SemaphoreType.DMA((devices,)),
         ],
         compiler_params=pltpu.CompilerParams(collective_id=0, has_side_effects=True),
         name="circuit",
     )(
-        gate_table(angles),
+        angles.T,
         marginal_qubits.reshape(1, marg_count),
-        state.reshape(2, rows, LANES),
+        state.reshape(2, rows, LANES).transpose(1, 0, 2).reshape(2 * rows, LANES),
         sample_high.reshape(samp_rows, LANES),
         sample_low.reshape(samp_rows, LANES),
     )

time: 48.5 us -> 46 us (0.948)
  local copies, waits for them, and re-layouts: 5.14 us -> 2.64 us
  Pallas kernels: 40.5 us -> 41.3 us
  other arithmetic: 0.75 us -> 0 us
    unnamed x4 -> x3, local copies, waits for them, and re-layouts: 3.04 us -> 1.38 us
    pallas_call x1, Pallas kernels: 40.5 us -> 41.3 us  [shards(): pl.pallas_call(functools.partial(kernel, sizes), out_shape=(jax.ShapeDtyp...]
    broadcast_in_dim x1 -> x0, local copies, waits for them, and re-layouts: 0.83 us -> none  [gate_table(): size = jnp.where((cell == 0) | (cell == 3), jnp.cos(theta), jnp.sin(theta))]
    mul x1 -> x0, other arithmetic: 0.73 us -> none  [gate_table(): return jnp.where(cell == 1, -1.0, 1.0) * size * turn]
where the time goes in v2:
time: 46 us; the launch traced here: 45.8 us
  Pallas kernels  41.3 us (90%)
  local copies, waits for them, and re-layouts  2.64 us (6%)
  between operations  1.81 us (4%)
    pallas_call x1, Pallas kernels, shards(): pl.pallas_call(functools.partial(kernel, sizes), out_shape=(jax.ShapeDtyp...  41.3 us
    unnamed x3, local copies, waits for them, and re-layouts  1.38 us
    dynamic_slice x1, local copies, waits for them, and re-layouts, shards(): lax.dynamic_slice_in_dim(hist.reshape(bins), position * per_device, per_d...  1.26 us

profile of v2, /device:TPU:0, one launch (start us, length us, event | category | flops | bytes accessed | tf_op | source)
XLA Modules:
  0.0 45.8 jit_solution(8649127751456107867)
XLA Ops:
  0.6 41.3 %circuit.1 = (f32[64,128]{1,0:T(8,128)}, f32[8,128]{1,0:T(8,128)}, f32[1,128]{1,0:T(1,128)}) custom-call(f32[3,20]{1,0:T(4,128)} %bitcast.17, s32[1,10]{1,0:T(1,128)} %bitcast.18, f32[512,128]{1,0:T(8,128)} %bitcast.13, s32[64,128]{1,0:T(8,128)} %bitcast.14, s32[64,128]{1,0:T(8,128)} %bitcast.15), custom_call_target="tpu_custom_call" | custom-call | tf_op jit(solution)/shard_map/circuit/pallas_call | solution.py:431
  42.0 1.3 %dynamic_slice.3 = f32[32]{0:T(128)} dynamic-slice(f32[1024]{0:T(1024)} %bitcast.19, s32[]{:T(128)S(6)} %select_n.3), dynamic_slice_sizes={32} | dynamic-slice | bytes 260 | tf_op jit(solution)/shard_map/dynamic_slice | solution.py:471
  43.3 0.0 copy-start
  43.3 1.4 %copy.11 = f32[8192]{0:T(1024)} copy(f32[8192]{0:T(1024)} %bitcast.16) | data formatting | bytes 65536
  44.6 0.0 copy-done
Async XLA Ops:
  43.3 1.4 %copy-start = (f32[1,128]{1,0:T(1,128)S(1)}, f32[1,128]{1,0:T(1,128)}, u32[]{:S(2)}) copy-start(f32[1,128]{1,0:T(1,128)} %get-tuple-element.8) | copy-start | bytes 1540

commit v3 on v2

--- a/solution.py
+++ b/solution.py
@@ -134,7 +134,7 @@
     return jnp.concatenate([top, rest], axis=0)
 
 
-def lookup(table, upper, lower):
+def lookup_dot(table, upper, lower):
     rows = upper.shape[0]
     count = table.shape[1]
     hot = jnp.concatenate([one_hot(upper[r : r + 1], count) for r in range(rows)], axis=1)
@@ -147,6 +147,30 @@
         value = jnp.where(lane_ids == lower[r : r + 1], value, 0.0)
         found.append(jnp.sum(value, axis=0, keepdims=True))
     return jnp.concatenate(found, axis=0)
+
+
+def lookup_lanes(table_ref, upper, lower):
+    rows = upper.shape[0]
+    if rows < SUBLANES:
+        upper = jnp.concatenate([upper] * (SUBLANES // rows), axis=0)
+        lower = jnp.concatenate([lower] * (SUBLANES // rows), axis=0)
+    shape = (SUBLANES, LANES)
+    bits = table_ref.shape[0].bit_length() - 1
+    high = [((upper >> bit) & 1) == 1 for bit in range(bits)]
+
+    def pick(first, bit):
+        if bit < 0:
+            line = jnp.broadcast_to(table_ref[first : first + 1], shape)
+            return jnp.take_along_axis(line, lower, axis=1, mode="promise_in_bounds")
+        zero = pick(first, bit - 1)
+        return jnp.where(high[bit], pick(first + (1 << bit), bit - 1), zero)
+
+    return pick(0, bits - 1)[:rows]
+
+
+def lookup_both(table, plain, wanted, other):
+    one = lookup_dot(table, wanted[0], wanted[1])
+    return one, lookup_lanes(plain, other[0], other[1])
 
 
 def kernel(
@@ -174,6 +198,8 @@
     code_ref,
     rank_ref,
     table_ref,
+    plain_ref,
+    back_ref,
     gates,
     sends,
     recvs,
@@ -362,36 +388,61 @@
 
     all_of(2, wt_in).wait_recv()
     spread(4, his_out, his_in)
-    table_ref[...] = split_table(join(wt_in[...]))
-
-    def answer(wanted):
-        return lookup(table_ref[...], wanted >> 7, wanted & (LANES - 1))
-
-    found = answer(req_out[me])
-    ans_in[me] = found
-
-    def reply(k, total):
+    plain_ref[...] = join(wt_in[...])
+    table_ref[...] = split_table(plain_ref[...])
+
+    def parts(wanted):
+        return wanted >> 7, wanted & (LANES - 1)
+
+    def answers(wanted, other):
+        found, second = lookup_both(
+            table_ref[:, 0:rows], plain_ref, parts(wanted), parts(other)
+        )
+        return found, jnp.where(other >= 0, second, 0.0)
+
+    def asked(k):
         source = peer(devices - k)
         ask(req_out.at[source], source, source).wait_recv()
-        found = answer(req_in[source])
+        return source
+
+    def send(source, found):
         ans_out[source] = found
         copy(3, ans_out.at[source], ans_in.at[me], source).start()
-        return total + jnp.sum(found, axis=0, keepdims=True)
-
-    total = lax.fori_loop(1, devices, reply, jnp.sum(found, axis=0, keepdims=True))
+
+    source = asked(1)
+    found, own = answers(req_in[source], req_out[me])
+    send(source, found)
+    ans_in[me] = own
+
+    def reply(t, total):
+        first, second = asked(2 * t), asked(2 * t + 1)
+        found, other = answers(req_in[first], req_in[second])
+        send(first, found)
+        send(second, other)
+        return total + jnp.sum(found + other, axis=0, keepdims=True)
+
+    total = jnp.sum(found + own, axis=0, keepdims=True)
+    total = lax.fori_loop(1, devices // 2, reply, total)
     tot_out[0, 0:1] = total
     tot_out[0, 1:2] = norm_part
     spread(5, tot_out, tot_in)
 
     all_of(3, ans_in).wait_recv()
-    table_ref[...] = split_table(join(ans_in[...]))
+    back_ref[...] = join(ans_in[...])
+    table_ref[:, 0:codes] = split_table(back_ref[...])
 
     def fetch(t, carry):
-        window = pl.ds(pl.multiple_of(t * SUBLANES, SUBLANES), SUBLANES)
-        probs_ref[window] = lookup(table_ref[...], code_ref[window], rank_ref[window])
+        one = pl.ds(pl.multiple_of(2 * t * SUBLANES, SUBLANES), SUBLANES)
+        two = pl.ds(pl.multiple_of((2 * t + 1) * SUBLANES, SUBLANES), SUBLANES)
+        probs_ref[one], probs_ref[two] = lookup_both(
+            table_ref[:, 0:codes],
+            back_ref,
+            (code_ref[one], rank_ref[one]),
+            (code_ref[two], rank_ref[two]),
+        )
         return carry
 
-    lax.fori_loop(0, steps, fetch, 0)
+    lax.fori_loop(0, steps // 2, fetch, 0)
     all_of(5, tot_in).wait_recv()
     all_of(4, his_in).wait_recv()
     sums = jnp.sum(jnp.sum(tot_in[...], axis=0), axis=1, keepdims=True)
@@ -453,6 +504,8 @@
             pltpu.VMEM((samp_rows, LANES), i32),
             pltpu.VMEM((samp_rows, LANES), i32),
             pltpu.VMEM((2 * LANES, max(rows, codes)), bf16),
+            pltpu.VMEM((rows, LANES), f32),
+            pltpu.VMEM((codes, LANES), f32),
             pltpu.VMEM((8, -(-angles.shape[0] // SUBLANES) * SUBLANES, LANES), f32),
             pltpu.SemaphoreType.DMA((6,)),
             pltpu.SemaphoreType.DMA((6,)),

time: 46 us -> 41.4 us (0.900)
  Pallas kernels: 41.3 us -> 36.7 us
    pallas_call x1, Pallas kernels: 41.3 us -> 36.7 us  [shards(): pl.pallas_call(functools.partial(kernel, sizes), out_shape=(jax.ShapeDtyp...]
where the time goes in v3:
time: 41.4 us; the launch traced here: 41.2 us
  Pallas kernels  36.7 us (89%)
  local copies, waits for them, and re-layouts  2.64 us (6%)
  between operations  1.81 us (4%)
    pallas_call x1, Pallas kernels, shards(): pl.pallas_call(functools.partial(kernel, sizes), out_shape=(jax.ShapeDtyp...  36.7 us
    unnamed x3, local copies, waits for them, and re-layouts  1.38 us
    dynamic_slice x1, local copies, waits for them, and re-layouts, shards(): lax.dynamic_slice_in_dim(hist.reshape(bins), position * per_device, per_d...  1.26 us

profile of v3, /device:TPU:0, one launch (start us, length us, event | category | flops | bytes accessed | tf_op | source)
XLA Modules:
  0.0 41.2 jit_solution(6391481965127363984)
XLA Ops:
  0.6 36.7 %circuit.1 = (f32[64,128]{1,0:T(8,128)}, f32[8,128]{1,0:T(8,128)}, f32[1,128]{1,0:T(1,128)}) custom-call(f32[3,20]{1,0:T(4,128)} %bitcast.17, s32[1,10]{1,0:T(1,128)} %bitcast.18, f32[512,128]{1,0:T(8,128)} %bitcast.13, s32[64,128]{1,0:T(8,128)} %bitcast.14, s32[64,128]{1,0:T(8,128)} %bitcast.15), custom_call_target="tpu_custom_call" | custom-call | tf_op jit(solution)/shard_map/circuit/pallas_call | solution.py:482
  37.4 1.3 %dynamic_slice.3 = f32[32]{0:T(128)} dynamic-slice(f32[1024]{0:T(1024)} %bitcast.19, s32[]{:T(128)S(6)} %select_n.3), dynamic_slice_sizes={32} | dynamic-slice | bytes 260 | tf_op jit(solution)/shard_map/dynamic_slice | solution.py:524
  38.6 0.0 copy-start
  38.6 1.4 %copy.11 = f32[8192]{0:T(1024)} copy(f32[8192]{0:T(1024)} %bitcast.16) | data formatting | bytes 65536
  40.0 0.0 copy-done
Async XLA Ops:
  38.6 1.4 %copy-start = (f32[1,128]{1,0:T(1,128)S(1)}, f32[1,128]{1,0:T(1,128)}, u32[]{:S(2)}) copy-start(f32[1,128]{1,0:T(1,128)} %get-tuple-element.8) | copy-start | bytes 1540

commit v4 on v3

--- a/solution.py
+++ b/solution.py
@@ -205,7 +205,7 @@
     recvs,
     req_recvs,
 ):
-    devices, depth, capacity_rows, marg_count, amps_total, samples = sizes
+    devices, depth, capacity_rows, marg_count = sizes
     me = lax.axis_index("dev")
     global_bits = devices.bit_length() - 1
     rows = state.shape[0] // 2
@@ -445,20 +445,29 @@
     lax.fori_loop(0, steps // 2, fetch, 0)
     all_of(5, tot_in).wait_recv()
     all_of(4, his_in).wait_recv()
-    sums = jnp.sum(jnp.sum(tot_in[...], axis=0), axis=1, keepdims=True)
-    total, norm = sums[0:1], sums[1:2]
-    probs_ref[...] = amps_total * (probs_ref[...] / norm)
-    hist_ref[...] = float(bins) * (jnp.sum(his_in[...], axis=0) / norm)
-    fid = amps_total * (total / norm) / samples - 1.0
-    fid_ref[...] = jnp.broadcast_to(fid, (1, LANES))
+    hist_ref[...] = jnp.sum(his_in[...], axis=0)
+    fid_ref[...] = jnp.sum(tot_in[...], axis=0)
 
     for channel, into in enumerate((amp_in, req_in, wt_in, ans_in, his_in, tot_in)):
         all_of(channel, into).wait_send()
 
 
+def finish(sizes, values, hist, totals, probs_ref, mine_ref, fid_ref):
+    amps_total, samples = sizes
+    bins, mine = float(hist.shape[0] * LANES), mine_ref.shape[1]
+    start = lax.axis_index("dev") * mine
+    sums = jnp.sum(totals[...], axis=1, keepdims=True)
+    total, norm = sums[0:1], sums[1:2]
+    probs_ref[...] = amps_total * (values[...] / norm)
+    line = hist[pl.ds(start // LANES, 1)]
+    line = jnp.broadcast_to(line, (SUBLANES, LANES))
+    line = pltpu.roll(line, (LANES - start % LANES) % LANES, 1)
+    mine_ref[...] = bins * (line[0:1, :mine] / norm)
+    fid_ref[...] = amps_total * (total / norm) / samples - 1.0
+
+
 def shards(state, angles, sample_high, sample_low, marginal_qubits):
     devices = lax.axis_size("dev")
-    position = lax.axis_index("dev")
     amps_local = state.shape[1]
     samp_local = sample_low.shape[0]
     marg_count = marginal_qubits.shape[0]
@@ -472,19 +481,17 @@
         depth,
         capacity_rows,
         marg_count,
-        float(amps_local * devices),
-        float(samp_local * devices),
     )
     vmem = pl.BlockSpec(memory_space=pltpu.VMEM)
     smem = pl.BlockSpec(memory_space=pltpu.SMEM)
     codes = devices * capacity_rows
     bin_rows = bins // LANES
-    probs, hist, fid = pl.pallas_call(
+    values, hist, totals = pl.pallas_call(
         functools.partial(kernel, sizes),
         out_shape=(
             jax.ShapeDtypeStruct((samp_rows, LANES), f32),
             jax.ShapeDtypeStruct((bin_rows, LANES), f32),
-            jax.ShapeDtypeStruct((1, LANES), f32),
+            jax.ShapeDtypeStruct((2, LANES), f32),
         ),
         in_specs=[smem, smem, vmem, vmem, vmem],
         out_specs=(vmem, vmem, vmem),
@@ -520,9 +527,18 @@
         sample_high.reshape(samp_rows, LANES),
         sample_low.reshape(samp_rows, LANES),
     )
-    per_device = bins // devices
-    mine = lax.dynamic_slice_in_dim(hist.reshape(bins), position * per_device, per_device)
-    return probs.reshape(samp_local), mine, fid[0, 0]
+    probs, mine, fid = pl.pallas_call(
+        functools.partial(finish, (float(amps_local * devices), float(samp_local * devices))),
+        out_shape=(
+            jax.ShapeDtypeStruct((samp_rows, LANES), f32),
+            jax.ShapeDtypeStruct((1, bins // devices), f32),
+            jax.ShapeDtypeStruct((1, 1), f32),
+        ),
+        in_specs=[vmem, vmem, vmem],
+        out_specs=(vmem, vmem, vmem),
+        name="finish",
+    )(values, hist, totals)
+    return probs.reshape(samp_local), mine.reshape(bins // devices), fid.reshape(())
 
 
 def solution(mesh):

time: 41.4 us -> 38.9 us (0.940)
  local copies, waits for them, and re-layouts: 2.64 us -> 0 us
  Pallas kernels: 36.7 us -> 38 us
  between operations: 1.81 us -> 0.64 us
    pallas_call x0 -> x1, Pallas kernels: none -> 1.47 us  [shards(): pl.pallas_call(functools.partial(finish, (float(amps_local * devices), fl...]
    unnamed x3 -> x0, local copies, waits for them, and re-layouts: 1.38 us -> none
    dynamic_slice x1 -> x0, local copies, waits for them, and re-layouts: 1.26 us -> none  [shards(): lax.dynamic_slice_in_dim(hist.reshape(bins), position * per_device, per_d...]
where the time goes in v4:
time: 38.9 us; the launch traced here: 38.7 us
  Pallas kernels  38 us (98%)
  between operations  0.64 us (2%)
    pallas_call x1, Pallas kernels, shards(): pl.pallas_call(functools.partial(kernel, sizes), out_shape=(jax.ShapeDtyp...  36.6 us
    pallas_call x1, Pallas kernels, shards(): pl.pallas_call(functools.partial(finish, (float(amps_local * devices), fl...  1.47 us

profile of v4, /device:TPU:0, one launch (start us, length us, event | category | flops | bytes accessed | tf_op | source)
XLA Modules:
  0.0 38.7 jit_solution(3168603102121272680)
XLA Ops:
  0.6 36.6 %circuit.1 = (f32[64,128]{1,0:T(8,128)}, f32[8,128]{1,0:T(8,128)}, f32[2,128]{1,0:T(2,128)}) custom-call(f32[3,20]{1,0:T(4,128)} %bitcast.15, s32[1,10]{1,0:T(1,128)} %bitcast.16, f32[512,128]{1,0:T(8,128)} %bitcast.12, s32[64,128]{1,0:T(8,128)} %bitcast.13, s32[64,128]{1,0:T(8,128)} %bitcast.14), custom_call_target="tpu_custom_call" | custom-call | tf_op jit(solution)/shard_map/circuit/pallas_call | solution.py:489
  37.2 1.5 %finish.1 = (f32[64,128]{1,0:T(8,128)}, f32[1,32]{1,0:T(1,128)}, f32[1,1]{1,0:T(1,128)}) custom-call(f32[64,128]{1,0:T(8,128)} %get-tuple-element.9.values, f32[8,128]{1,0:T(8,128)} %get-tuple-element.10.hist, f32[2,128]{1,0:T(2,128)} %get-tuple-element.11.totals), custom_call_target="tpu_custom_call" | custom-call | tf_op jit(solution)/shard_map/finish/pallas_call | solution.py:530

commit v5 on v4

--- a/solution.py
+++ b/solution.py
@@ -229,7 +229,7 @@
     def scatter(channel, out, into):
         @pl.loop(1, devices)
         def _(k):
-            target = peer(k)
+            target = peer(1 + lax.rem(k + devices // 3, devices - 1))
             copy(channel, out.at[target], into.at[me], target).start()
 
         into[me] = out[me]
@@ -347,11 +347,6 @@
     weight = xr * xr + xi * xi
     wt_out[...] = weight
     scatter(2, wt_out, wt_in)
-
-    @pl.loop(1, devices)
-    def _(k):
-        target = peer(k)
-        ask(req_out.at[target], me, target).start()
 
     weight = join(weight)
     norm_part = jnp.sum(weight, axis=0, keepdims=True)
@@ -385,6 +380,11 @@
         picked = jnp.where(row_code == bin_id - lane_part, folded, 0.0)
         his_out[0, pl.ds(c, 1)] = jnp.sum(picked, axis=0, keepdims=True)
 
+
+    @pl.loop(1, devices)
+    def _(k):
+        target = peer(k)
+        ask(req_out.at[target], me, target).start()
 
     all_of(2, wt_in).wait_recv()
     spread(4, his_out, his_in)

time: 38.9 us -> 37.4 us (0.961)
  Pallas kernels: 38 us -> 36.6 us
    pallas_call x1, Pallas kernels: 36.6 us -> 35.1 us  [shards(): pl.pallas_call(functools.partial(kernel, sizes), out_shape=(jax.ShapeDtyp...]
where the time goes in v5:
time: 37.4 us; the launch traced here: 37.2 us
  Pallas kernels  36.6 us (98%)
  between operations  0.64 us (2%)
    pallas_call x1, Pallas kernels, shards(): pl.pallas_call(functools.partial(kernel, sizes), out_shape=(jax.ShapeDtyp...  35.1 us
    pallas_call x1, Pallas kernels, shards(): pl.pallas_call(functools.partial(finish, (float(amps_local * devices), fl...  1.47 us

profile of v5, /device:TPU:0, one launch (start us, length us, event | category | flops | bytes accessed | tf_op | source)
XLA Modules:
  0.0 37.2 jit_solution(9009609424723011026)
XLA Ops:
  0.6 35.1 %circuit.1 = (f32[64,128]{1,0:T(8,128)}, f32[8,128]{1,0:T(8,128)}, f32[2,128]{1,0:T(2,128)}) custom-call(f32[3,20]{1,0:T(4,128)} %bitcast.15, s32[1,10]{1,0:T(1,128)} %bitcast.16, f32[512,128]{1,0:T(8,128)} %bitcast.12, s32[64,128]{1,0:T(8,128)} %bitcast.13, s32[64,128]{1,0:T(8,128)} %bitcast.14), custom_call_target="tpu_custom_call" | custom-call | tf_op jit(solution)/shard_map/circuit/pallas_call | solution.py:489
  35.8 1.5 %finish.1 = (f32[64,128]{1,0:T(8,128)}, f32[1,32]{1,0:T(1,128)}, f32[1,1]{1,0:T(1,128)}) custom-call(f32[64,128]{1,0:T(8,128)} %get-tuple-element.9.values, f32[8,128]{1,0:T(8,128)} %get-tuple-element.10.hist, f32[2,128]{1,0:T(2,128)} %get-tuple-element.11.totals), custom_call_target="tpu_custom_call" | custom-call | tf_op jit(solution)/shard_map/finish/pallas_call | solution.py:530
